TPU v7x, 32 devices: a whole 2x2x4 slice. The times are simulated.
32 devices in a mesh: section: 8 (over z, y), state: 4 (over x, core).
Axes of the slice: x: 2, y: 2, z: 4, core: 2. Of those that a mesh axis runs over, the one named last changes fastest.
Arguments:
- initial_state: float32 [32, 1024], P('state'), may hold values from -6 to 6
- state_ref: float32 [192, 32, 1024], P('section', 'state'), may hold values from -6 to 6
- state_weight: float32 [192, 32, 1024], P('section', 'state'), may hold values from 0.2 to 5
- input_matrix: bfloat16 [32, 1024, 512], P('state'), may hold values from -0.25 to 0.25
- kkt_inverse: float32 [512, 512], replicated, may hold values from -1 to 1, as said below
- input_bound: float32 [512], replicated, may hold values from 0.02 to 0.3
Outputs:
- states: float32 [192, 32, 1024], P('section', 'state')
- boxed: float32 [192, 512], P('section')
- dual_vars: float32 [192, 32, 1024], P('section', 'state')
- history: float32 [10, 2], replicated
Inputs may be any that keep to these rules, and one draw needn't show every extreme that they name: `kkt_inverse`: a symmetric matrix.
All inputs are finite; a program needn't handle non-finite values.
Results may differ from a plain program's by a relative error of at most 0.003.
Values may be sent and summed in bfloat16 or wider, within the bound.
No kernel may reach another device: no remote copies, remote signals or barrier semaphores. Data moves between devices by JAX's collectives and lax.ppermute only.
A program may use at most 128 MiB of HBM per device.

v0:
```python
import jax
import jax.numpy as jnp
from jax import lax
from jax.sharding import PartitionSpec as P

GX = 32
GY = 32
GZ = 32
ITERS = 10
diffusion = 0.15
epsilon = 1e-06


def with_halo(block, sides, width):
    for axis, dim in sides:
        count = lax.axis_size(axis)
        forward = [(i, i + 1) for i in range(count - 1)]
        backward = [(target, source) for source, target in forward]
        low = lax.ppermute(
            lax.slice_in_dim(block, block.shape[dim] - width, None, axis=dim), axis, forward
        )
        high = lax.ppermute(lax.slice_in_dim(block, 0, width, axis=dim), axis, backward)
        block = jnp.concatenate([low, block, high], axis=dim)
    return block


def passed_along(value, axis, steps):
    count = lax.axis_size(axis)
    leading, last = (max(0, -steps), min(count, count - steps))
    return lax.ppermute(value, axis, [(source, source + steps) for source in range(leading, last)])


def stencil(padded):
    centre = padded[:, 1:-1]
    across = padded[:, 2:] + padded[:, :-2]
    depth = centre.shape[-1]
    flat_pad = jnp.pad(centre, ((0, 0), (0, 0), (GZ, GZ)))
    along_y = flat_pad[:, :, 2 * GZ :] + flat_pad[:, :, : -2 * GZ]
    lower_z = jnp.pad(centre, ((0, 0), (0, 0), (1, 0)))[:, :, :-1]
    upper_z = jnp.pad(centre, ((0, 0), (0, 0), (0, 1)))[:, :, 1:]
    z_index = jnp.arange(depth) % GZ
    along_z = jnp.where(z_index > 0, lower_z, 0.0) + jnp.where(z_index < GZ - 1, upper_z, 0.0)
    return centre + diffusion * (across + along_y + along_z - 6.0 * centre)


def apply_rows(inputs_low, matrix):
    return lax.dot_general(
        inputs_low, matrix, (((1,), (1,)), ((), ())), preferred_element_type=jnp.float32
    )


def local(initial_state, state_ref, state_weight, input_matrix, kkt_inverse, input_bound):
    section_count, planes, plane_size = state_ref.shape
    input_width = input_matrix.shape[2]
    matrix = input_matrix.reshape(planes * plane_size, input_width)
    penalty = float(GX * GY * GZ) / input_width
    is_first = lax.axis_index("section") == 0
    groups = lax.axis_size("state")
    state_seat = lax.axis_index("state")
    cell_count = section_count * lax.axis_size("section") * GX * GY * GZ
    input_count = section_count * lax.axis_size("section") * input_width
    states = jnp.zeros_like(state_ref)
    dual_vars = jnp.zeros_like(state_ref)
    boxed = jnp.zeros((section_count, input_width), jnp.float32)
    scaled = jnp.zeros((section_count, input_width), jnp.float32)
    wide_matrix = with_halo(input_matrix, (("state", 0),), 1).reshape(-1, input_width)
    plane_index = jnp.arange(planes + 2)[:, None]
    outside = (plane_index == 0) & (state_seat == 0) | (plane_index == planes + 1) & (
        state_seat == groups - 1
    )
    rim_mask = jnp.where(outside, 0.0, 1.0).astype(jnp.float32)
    history = []
    for iteration in range(ITERS):
        last_state = passed_along(states[-1], "section", 1)
        prior = jnp.where(is_first, initial_state, last_state)
        joined = jnp.concatenate([prior[None], states, dual_vars], 0)
        padded = with_halo(joined, (("state", 1),), 2)
        moved_wide = stencil(padded[:section_count])
        states_wide = padded[1 : section_count + 1, 1:-1]
        duals_wide = padded[section_count + 1 :, 1:-1]
        target_wide = states_wide - moved_wide + duals_wide
        moved_prior = moved_wide[:, 1:-1]
        target = target_wide[:, 1:-1]
        target_low = target.astype(jnp.bfloat16).reshape(section_count, -1)
        partial_pull = jnp.dot(target_low, matrix, preferred_element_type=jnp.float32)
        pulled = lax.psum(partial_pull, "state")
        rhs_rows = pulled + penalty * (boxed - scaled)
        inputs = jnp.dot(rhs_rows, kkt_inverse, precision=lax.Precision.HIGHEST)
        inputs_low = inputs.astype(jnp.bfloat16)
        driven_wide = apply_rows(inputs_low, wide_matrix).reshape(
            section_count, planes + 2, plane_size
        )
        defect_wide = (target_wide - driven_wide) * rim_mask
        driven = driven_wide[:, 1:-1]
        defect = defect_wide[:, 1:-1]
        following = passed_along(defect_wide[0], "section", -1)
        ahead_defect = jnp.concatenate([defect_wide[1:], following[None]], 0)
        back_term = stencil(ahead_defect)
        updated = (state_weight * state_ref + (states - defect) + back_term + states) / (
            state_weight + 2.0
        )
        primal = updated - moved_prior - driven
        dual_vars = dual_vars + primal
        boxed_new = jnp.clip(inputs + scaled, -input_bound, input_bound)
        box_gap = inputs - boxed_new
        scaled = scaled + box_gap
        boxed = boxed_new
        states = updated
        primal_square = jnp.sum(primal * primal)
        gap_square = jnp.sum(box_gap * box_gap) / groups
        totals = lax.psum((primal_square, gap_square), ("section", "state"))
        history.append(
            jnp.stack(
                [
                    jnp.sqrt(totals[0] / cell_count + epsilon),
                    jnp.sqrt(totals[1] / input_count + epsilon),
                ]
            )
        )
    record = jnp.stack(history)
    return (states, boxed, dual_vars, record)


def solution(mesh):
    return jax.shard_map(
        local,
        mesh=mesh,
        in_specs=(
            P("state", None),
            P("section", "state", None),
            P("section", "state", None),
            P("state", None, None),
            P(),
            P(),
        ),
        out_specs=(
            P("section", "state", None),
            P("section", None),
            P("section", "state", None),
            P(),
        ),
        check_vma=False,
    )
```

profile of v0, /device:TPU:12, one launch (start us, length us, event | category | flops | bytes accessed | tf_op | source)
XLA Modules:
  0.0 624.9 jit_solution(1933036389020178397)
XLA Ops:
  0.7 3.6 collective-permute-start
  14.2 4.0 collective-permute-start.3
  25.3 14.3 %psum.210 = f32[24,512]{1,0:T(8,128)S(1)} all-reduce(f32[24,512]{1,0:T(8,128)S(1)} %convolution_bitcast_fusion.9), channel_id=1, replica_groups=mesh['section'=8,'state'=4] {'state'}, use_global_device_ids=true, to_apply=%region_0.1 | all-reduce | flops 12288 | bytes 98304 | tf_op jit(solution)/shard_map/psum | solution.py:86
  42.5 7.3 %constant_dynamic-update-slice_fusion.1 = bf16[10,1024,512]{2,1,0:T(8,128)(2,1)} fusion(bf16[10,1024,512]{2,1,0:T(8,128)(2,1)} %constant_dynamic-update-slice_fusion.2, bf16[8,1024,512]{2,1,0:T(8,128)(2,1)} %param.9), kind=kLoop, calls=%fused_computation.746 | loop fusion | bytes 16777216
  52.1 6.9 %fusion.342 = f32[24,10,1024]{2,0,1:T(8,128)S(1)} fusion(bf16[10,1024,512]{2,1,0:T(8,128)(2,1)} %constant_dynamic-update-slice_fusion, f32[24,512]{1,0:T(8,128)S(1)} %fusion.421), kind=kOutput, calls=%fused_computation.705 | convolution fusion | flops 251670528 | bytes 11517952 | tf_op jit(solution)/shard_map/dot_general | solution.py:47
  59.9 3.3 collective-permute-start.5
  69.3 3.6 collective-permute-start.6
  82.0 3.3 slice_add_fusion.3
  88.2 16.2 %psum.211 = f32[24,512]{1,0:T(8,128)} all-reduce(f32[24,512]{1,0:T(8,128)S(1)} %convolution_bitcast_fusion.8), channel_id=1, replica_groups=mesh['section'=8,'state'=4] {'state'}, use_global_device_ids=true, to_apply=%region_1.2 | all-reduce | flops 12288 | bytes 98304 | tf_op jit(solution)/shard_map/psum | solution.py:86
  106.4 6.9 %fusion.340 = f32[24,10,1024]{2,0,1:T(8,128)S(1)} fusion(bf16[10,1024,512]{2,1,0:T(8,128)(2,1)} %constant_dynamic-update-slice_fusion, f32[24,512]{1,0:T(8,128)S(1)} %get-tuple-element.121), kind=kOutput, calls=%fused_computation.703 | convolution fusion | flops 251670528 | bytes 11517952 | tf_op jit(solution)/shard_map/dot_general | solution.py:47
  114.3 3.3 collective-permute-start.9
  117.8 3.9 collective-permute-done.9
  124.7 3.4 collective-permute-start.10
  132.1 3.5 collective-permute-start.11
  137.3 3.3 slice_add_fusion.2
  143.5 15.6 %psum.212 = f32[24,512]{1,0:T(8,128)S(1)} all-reduce(f32[24,512]{1,0:T(8,128)S(1)} %convolution_bitcast_fusion.7), channel_id=1, replica_groups=mesh['section'=8,'state'=4] {'state'}, use_global_device_ids=true, to_apply=%region_2.3 | all-reduce | flops 12288 | bytes 98304 | tf_op jit(solution)/shard_map/psum | solution.py:86
  159.8 6.9 %fusion.338 = f32[24,10,1024]{2,0,1:T(8,128)S(1)} fusion(bf16[10,1024,512]{2,1,0:T(8,128)(2,1)} %constant_dynamic-update-slice_fusion, f32[24,512]{1,0:T(8,128)S(1)} %fusion.297), kind=kOutput, calls=%fused_computation.701 | convolution fusion | flops 251670528 | bytes 11517952 | tf_op jit(solution)/shard_map/dot_general | solution.py:47
  167.6 3.3 collective-permute-start.13
  171.1 3.9 collective-permute-done.13
  178.0 3.4 collective-permute-start.14
  185.4 3.2 collective-permute-start.15
  190.7 3.3 slice_add_fusion.1
  197.5 16.8 %psum.213 = f32[24,512]{1,0:T(8,128)} all-reduce(f32[24,512]{1,0:T(8,128)} %convolution_bitcast_fusion.6), channel_id=1, replica_groups=mesh['section'=8,'state'=4] {'state'}, use_global_device_ids=true, to_apply=%region_3.4 | all-reduce | flops 12288 | bytes 98304 | tf_op jit(solution)/shard_map/psum | solution.py:86
  216.3 6.9 %fusion.336 = f32[24,10,1024]{2,0,1:T(8,128)S(1)} fusion(bf16[10,1024,512]{2,1,0:T(8,128)(2,1)} %constant_dynamic-update-slice_fusion, f32[24,512]{1,0:T(8,128)S(1)} %get-tuple-element.123), kind=kOutput, calls=%fused_computation.699 | convolution fusion | flops 251670528 | bytes 11517952 | tf_op jit(solution)/shard_map/dot_general | solution.py:47
  224.2 3.3 collective-permute-start.17
  227.7 3.9 collective-permute-done.17
  234.5 3.4 collective-permute-start.18
  241.9 3.3 collective-permute-start.19
  247.2 3.3 slice_add_fusion
  253.3 15.6 %psum.214 = f32[24,512]{1,0:T(8,128)S(1)} all-reduce(f32[24,512]{1,0:T(8,128)S(1)} %convolution_bitcast_fusion.5), channel_id=1, replica_groups=mesh['section'=8,'state'=4] {'state'}, use_global_device_ids=true, to_apply=%region_4.5 | all-reduce | flops 12288 | bytes 98304 | tf_op jit(solution)/shard_map/psum | solution.py:86
  269.6 6.9 %fusion.334 = f32[24,10,1024]{2,0,1:T(8,128)S(1)} fusion(bf16[10,1024,512]{2,1,0:T(8,128)(2,1)} %constant_dynamic-update-slice_fusion, f32[24,512]{1,0:T(8,128)S(1)} %fusion.289), kind=kOutput, calls=%fused_computation.697 | convolution fusion | flops 251670528 | bytes 11517952 | tf_op jit(solution)/shard_map/dot_general | solution.py:47
  277.4 3.3 collective-permute-start.21
  280.9 3.9 collective-permute-done.21
  289.3 3.4 collective-permute-start.22
  296.6 3.7 collective-permute-start.23
  306.1 17.3 %psum.215 = f32[24,512]{1,0:T(8,128)} all-reduce(f32[24,512]{1,0:T(8,128)} %convolution_bitcast_fusion.4), channel_id=1, replica_groups=mesh['section'=8,'state'=4] {'state'}, use_global_device_ids=true, to_apply=%region_5.6 | all-reduce | flops 12288 | bytes 98304 | tf_op jit(solution)/shard_map/psum | solution.py:86
  325.6 7.6 %subtract_multiply_fusion.8 = (f32[24,10,1024]{2,0,1:T(8,128)S(1)}, f32[24,10,1024]{2,0,1:T(8,128)S(1)}) fusion(f32[10]{0:T(128)} %copy-done.88, f32[49,12,1024]{2,0,1:T(8,128)} %copy-done.33, f32[24,10,1024]{2,0,1:T(8,128)S(1)} %copy-done.7, bf16[10,1024,512]{2,1,0:T(8,128)(2,1)} %constant_dynamic-update-slice_fusion, f32[24,512]{1,0:T(8,128)S(1)} %get-tuple-element.127), kind=kOutput, calls=%fused_computation.278 | convolution fusion | flops 252653568 | bytes 15450152 | tf_op jit(solution)/shard_map/dot_general | solution.py:47
  333.2 3.4 collective-permute-start.25
  336.8 4.0 collective-permute-done.25
  343.3 3.4 collective-permute-start.26
  350.6 3.3 collective-permute-start.27
  359.6 16.3 %psum.216 = f32[24,512]{1,0:T(8,128)S(1)} all-reduce(f32[24,512]{1,0:T(8,128)S(1)} %convolution_bitcast_fusion.3), channel_id=1, replica_groups=mesh['section'=8,'state'=4] {'state'}, use_global_device_ids=true, to_apply=%region_6.7 | all-reduce | flops 12288 | bytes 98304 | tf_op jit(solution)/shard_map/psum | solution.py:86
  377.2 7.5 %subtract_multiply_fusion.7 = (f32[24,10,1024]{2,0,1:T(8,128)S(1)}, f32[24,10,1024]{2,0,1:T(8,128)S(1)}) fusion(f32[10]{0:T(128)S(1)} %copy-done.93, f32[49,12,1024]{2,0,1:T(8,128)} %copy-done.35, f32[24,10,1024]{2,0,1:T(8,128)S(1)} %copy-done.11, bf16[10,1024,512]{2,1,0:T(8,128)(2,1)} %constant_dynamic-update-slice_fusion, f32[24,512]{1,0:T(8,128)S(1)} %fusion.281), kind=kOutput, calls=%fused_computation.277 | convolution fusion | flops 252653568 | bytes 15450152 | tf_op jit(solution)/shard_map/dot_general | solution.py:47
  384.8 3.4 collective-permute-start.29
  388.4 3.9 collective-permute-done.29
  394.6 3.4 collective-permute-start.30
  401.9 3.3 collective-permute-start.31
  411.5 17.3 %psum.217 = f32[24,512]{1,0:T(8,128)} all-reduce(f32[24,512]{1,0:T(8,128)} %convolution_bitcast_fusion.2), channel_id=1, replica_groups=mesh['section'=8,'state'=4] {'state'}, use_global_device_ids=true, to_apply=%region_7.8 | all-reduce | flops 12288 | bytes 98304 | tf_op jit(solution)/shard_map/psum | solution.py:86
  431.0 7.6 %subtract_multiply_fusion.6 = (f32[24,10,1024]{2,0,1:T(8,128)S(1)}, f32[24,10,1024]{2,0,1:T(8,128)S(1)}) fusion(f32[10]{0:T(128)} %copy-done.88, f32[49,12,1024]{2,0,1:T(8,128)} %copy-done.34, f32[24,10,1024]{2,0,1:T(8,128)S(1)} %copy-done.9, bf16[10,1024,512]{2,1,0:T(8,128)(2,1)} %constant_dynamic-update-slice_fusion, f32[24,512]{1,0:T(8,128)S(1)} %get-tuple-element.133), kind=kOutput, calls=%fused_computation.276 | convolution fusion | flops 252653568 | bytes 15450152 | tf_op jit(solution)/shard_map/dot_general | solution.py:47
  438.6 3.3 collective-permute-start.33
  442.0 4.0 collective-permute-done.33
  448.3 3.6 collective-permute-start.34
  455.9 3.1 collective-permute-start.35
  464.6 16.2 %psum.218 = f32[24,512]{1,0:T(8,128)S(1)} all-reduce(f32[24,512]{1,0:T(8,128)S(1)} %convolution_bitcast_fusion.1), channel_id=1, replica_groups=mesh['section'=8,'state'=4] {'state'}, use_global_device_ids=true, to_apply=%region_8.9 | all-reduce | flops 12288 | bytes 98304 | tf_op jit(solution)/shard_map/psum | solution.py:86
  482.0 7.5 %subtract_multiply_fusion.5 = (f32[24,10,1024]{2,0,1:T(8,128)S(1)}, f32[24,10,1024]{2,0,1:T(8,128)S(1)}) fusion(f32[10]{0:T(128)S(1)} %copy-done.94, f32[49,12,1024]{2,0,1:T(8,128)} %copy-done.36, f32[24,10,1024]{2,0,1:T(8,128)S(1)} %copy-done.13, bf16[10,1024,512]{2,1,0:T(8,128)(2,1)} %constant_dynamic-update-slice_fusion, f32[24,512]{1,0:T(8,128)S(1)} %fusion.273), kind=kOutput, calls=%fused_computation.275 | convolution fusion | flops 252653568 | bytes 15450152 | tf_op jit(solution)/shard_map/dot_general | solution.py:47
  489.6 3.4 collective-permute-start.37
  493.1 4.0 collective-permute-done.37
  499.4 3.4 collective-permute-start.38
  516.2 17.7 %psum.219 = f32[24,512]{1,0:T(8,128)} all-reduce(f32[24,512]{1,0:T(8,128)} %convolution_bitcast_fusion), channel_id=1, replica_groups=mesh['section'=8,'state'=4] {'state'}, use_global_device_ids=true, to_apply=%region_9.10 | all-reduce | flops 12288 | bytes 98304 | tf_op jit(solution)/shard_map/psum | solution.py:86
  533.8 3.2 multiply_reduce_fusion.12
  537.0 8.5 %subtract_multiply_fusion.4 = (f32[24,10,1024]{2,0,1:T(8,128)S(1)}, f32[24,10,1024]{2,0,1:T(8,128)}) fusion(f32[10]{0:T(128)S(1)} %copy-done.95, f32[49,12,1024]{2,0,1:T(8,128)} %copy-done.37, f32[24,10,1024]{2,0,1:T(8,128)S(1)} %copy-done.15, bf16[10,1024,512]{2,1,0:T(8,128)(2,1)} %constant_dynamic-update-slice_fusion, ...), kind=kOutput, calls=%fused_computation.274 | convolution fusion | flops 252641280 | bytes 15425576 | tf_op jit(solution)/shard_map/dot_general | solution.py:47
  545.5 3.3 collective-permute-start.41
  558.3 3.8 multiply_reduce_fusion
  565.0 43.7 %all-reduce.61 = (f32[]{:T(128)}, f32[]{:T(128)}, f32[]{:T(128)}, f32[]{:T(128)}, f32[]{:T(128)}, /*index=5*/f32[]{:T(128)}, f32[]{:T(128)}, f32[]{:T(128)}, f32...) all-reduce(f32[]{:T(128)S(6)} %div.131, ...), channel_id=1, replica_groups=mesh['section'=8,'state'=4] {'section','state'}, use_global_device_ids=true, to_apply=%region_13.14 | all-reduce | flops 20 | bytes 160 | tf_op jit(solution)/shard_map/psum | solution.py:111
  (480 shorter events, 166.9 us)
Async XLA Ops:
  0.6 39.0 %copy-start = (f32[512,512]{1,0:T(8,128)S(1)}, f32[512,512]{1,0:T(8,128)}, u32[]{:S(2)}) copy-start(f32[512,512]{1,0:T(8,128)} %param.10) | copy-start | bytes 3145732
  0.7 5.9 collective-permute-start
  6.8 12.9 %collective-permute-start.2 = (f32[49,2,1024]{2,1,0:T(2,128)S(1)}, f32[49,2,1024]{2,1,0:T(2,128)S(1)}, u32[]{:S(2)}, u32[]{:S(2)}) collective-permute-start(f32[49,2,1024]{2,1,0:T(2,128)S(1)} %get-tuple-element.119), channel_id=1, source_target_pairs={{1,0},{2,1},{3,2},{5,4},{6,5},{7,6},{9,8},{10,9},{11,10},{13,12},{... | collective-permute-start | bytes 1204232 | tf_op jit(solution)/shard_map/ppermute | solution.py:22
  8.1 11.6 %collective-permute-start.1 = (f32[49,2,1024]{2,1,0:T(2,128)S(1)}, f32[49,2,1024]{2,1,0:T(2,128)S(1)}, u32[]{:S(2)}, u32[]{:S(2)}) collective-permute-start(f32[49,2,1024]{2,1,0:T(2,128)S(1)} %get-tuple-element.118), channel_id=1, source_target_pairs={{0,1},{1,2},{2,3},{4,5},{5,6},{6,7},{8,9},{9,10},{10,11},{12,13},{... | collective-permute-start | bytes 1204232 | tf_op jit(solution)/shard_map/ppermute | solution.py:19
  14.2 26.1 %collective-permute-start.3 = (bf16[1,1024,512]{2,1,0:T(8,128)(2,1)}, bf16[1,1024,512]{2,1,0:T(8,128)(2,1)}, u32[]{:S(2)}, u32[]{:S(2)}) collective-permute-start(bf16[1,1024,512]{2,1,0:T(8,128)(2,1)} %get-tuple-element.86), channel_id=1, source_target_pairs={{0,1},{1,2},{2,3},{4,5},{5,6},{6,7},{8,9},{9,10},{10,11},{12,13},{... | collective-permute-start | bytes 3145736 | tf_op jit(solution)/shard_map/ppermute | solution.py:19
  18.2 31.6 %collective-permute-start.4 = (bf16[1,1024,512]{2,1,0:T(8,128)(2,1)}, bf16[1,1024,512]{2,1,0:T(8,128)(2,1)}, u32[]{:S(2)}, u32[]{:S(2)}) collective-permute-start(bf16[1,1024,512]{2,1,0:T(8,128)(2,1)} %get-tuple-element.85), channel_id=1, source_target_pairs={{1,0},{2,1},{3,2},{5,4},{6,5},{7,6},{9,8},{10,9},{11,10},{13,12},{... | collective-permute-start | bytes 3145736 | tf_op jit(solution)/shard_map/ppermute | solution.py:22
  19.5 39.5 %copy-start.88 = (f32[10]{0:T(128)}, f32[10]{0:T(128)S(1)}, u32[]{:S(2)}) copy-start(f32[10]{0:T(128)S(1)} %or_select_fusion) | copy-start | bytes 124
  59.9 7.5 %collective-permute-start.5 = (f32[10,1024]{1,0:T(8,128)S(1)}, f32[10,1024]{1,0:T(8,128)S(1)}, u32[]{:S(2)}, u32[]{:S(2)}) collective-permute-start(f32[10,1024]{1,0:T(8,128)S(1)} %slice_bitcast_fusion.4), channel_id=1, source_target_pairs={{4,0},{8,4},{12,8},{16,12},{20,16},{24,20},{28,24},{5,1},{9,5},{13... | collective-permute-start | bytes 122888 | tf_op jit(solution)/shard_map/ppermute | solution.py:30
  69.3 5.8 collective-permute-start.6
  75.4 4.4 collective-permute-start.8
  76.7 4.4 collective-permute-start.7
  114.3 7.4 %collective-permute-start.9 = (f32[10,1024]{1,0:T(8,128)S(1)}, f32[10,1024]{1,0:T(8,128)S(1)}, u32[]{:S(2)}, u32[]{:S(2)}) collective-permute-start(f32[10,1024]{1,0:T(8,128)S(1)} %slice_bitcast_fusion.3), channel_id=1, source_target_pairs={{4,0},{8,4},{12,8},{16,12},{20,16},{24,20},{28,24},{5,1},{9,5},{13... | collective-permute-start | bytes 122888 | tf_op jit(solution)/shard_map/ppermute | solution.py:30
  124.7 5.8 collective-permute-start.10
  130.8 4.8 collective-permute-start.12
  132.1 4.4 collective-permute-start.11
  142.0 17.1 %copy-start.66 = (f32[24,512]{1,0:T(8,128)S(1)}, f32[24,512]{1,0:T(8,128)}, u32[]{:S(2)}) copy-start(f32[24,512]{1,0:T(8,128)} %get-tuple-element.120) | copy-start | bytes 147460
  142.0 17.1 %copy-start.77 = (f32[24,512]{1,0:T(8,128)S(1)}, f32[24,512]{1,0:T(8,128)}, u32[]{:S(2)}) copy-start(f32[24,512]{1,0:T(8,128)} %copy-done.76) | copy-start | bytes 147460
  167.6 7.4 %collective-permute-start.13 = (f32[10,1024]{1,0:T(8,128)S(1)}, f32[10,1024]{1,0:T(8,128)S(1)}, u32[]{:S(2)}, u32[]{:S(2)}) collective-permute-start(f32[10,1024]{1,0:T(8,128)S(1)} %slice_bitcast_fusion.2), channel_id=1, source_target_pairs={{4,0},{8,4},{12,8},{16,12},{20,16},{24,20},{28,24},{5,1},{9,5},{13... | collective-permute-start | bytes 122888 | tf_op jit(solution)/shard_map/ppermute | solution.py:30
  178.0 5.8 collective-permute-start.14
  184.1 4.5 collective-permute-start.16
  185.4 4.4 collective-permute-start.15
  224.2 7.4 %collective-permute-start.17 = (f32[10,1024]{1,0:T(8,128)S(1)}, f32[10,1024]{1,0:T(8,128)S(1)}, u32[]{:S(2)}, u32[]{:S(2)}) collective-permute-start(f32[10,1024]{1,0:T(8,128)S(1)} %slice_bitcast_fusion.1), channel_id=1, source_target_pairs={{4,0},{8,4},{12,8},{16,12},{20,16},{24,20},{28,24},{5,1},{9,5},{13... | collective-permute-start | bytes 122888 | tf_op jit(solution)/shard_map/ppermute | solution.py:30
  234.5 5.8 collective-permute-start.18
  240.6 4.6 collective-permute-start.20
  241.9 4.4 collective-permute-start.19
  251.8 17.1 %copy-start.67 = (f32[24,512]{1,0:T(8,128)S(1)}, f32[24,512]{1,0:T(8,128)}, u32[]{:S(2)}) copy-start(f32[24,512]{1,0:T(8,128)} %get-tuple-element.120) | copy-start | bytes 147460
  251.8 17.1 %copy-start.72 = (f32[24,512]{1,0:T(8,128)S(1)}, f32[24,512]{1,0:T(8,128)}, u32[]{:S(2)}) copy-start(f32[24,512]{1,0:T(8,128)} %get-tuple-element.122) | copy-start | bytes 147460
  251.8 17.1 %copy-start.79 = (f32[24,512]{1,0:T(8,128)S(1)}, f32[24,512]{1,0:T(8,128)}, u32[]{:S(2)}) copy-start(f32[24,512]{1,0:T(8,128)} %copy-done.78) | copy-start | bytes 147460
  277.4 7.4 %collective-permute-start.21 = (f32[10,1024]{1,0:T(8,128)S(1)}, f32[10,1024]{1,0:T(8,128)S(1)}, u32[]{:S(2)}, u32[]{:S(2)}) collective-permute-start(f32[10,1024]{1,0:T(8,128)S(1)} %slice_bitcast_fusion), channel_id=1, source_target_pairs={{4,0},{8,4},{12,8},{16,12},{20,16},{24,20},{28,24},{5,1},{9,5},{13... | collective-permute-start | bytes 122888 | tf_op jit(solution)/shard_map/ppermute | solution.py:30
  289.3 5.8 collective-permute-start.22
  295.3 5.1 collective-permute-start.24
  296.6 4.7 collective-permute-start.23
  333.2 7.6 %collective-permute-start.25 = (f32[10,1024]{1,0:T(8,128)S(1)}, f32[10,1024]{1,0:T(8,128)S(1)}, u32[]{:S(2)}, u32[]{:S(2)}) collective-permute-start(f32[10,1024]{1,0:T(8,128)S(1)} %bitcast.237), channel_id=1, source_target_pairs={{4,0},{8,4},{12,8},{16,12},{20,16},{24,20},{28,24},{5,1},{9,5},{13... | collective-permute-start | bytes 122888 | tf_op jit(solution)/shard_map/ppermute | solution.py:30
  343.3 12.7 %copy-start.2 = (f32[24,8,1024]{2,0,1:T(8,128)}, f32[24,8,1024]{2,0,1:T(8,128)S(1)}, u32[]{:S(2)}) copy-start(f32[24,8,1024]{2,0,1:T(8,128)S(1)} %get-tuple-element.59) | copy-start | bytes 2359300
  343.3 5.8 collective-permute-start.26
  349.3 4.6 collective-permute-start.28
  350.6 4.7 collective-permute-start.27
  358.3 17.6 %copy-start.69 = (f32[24,512]{1,0:T(8,128)S(1)}, f32[24,512]{1,0:T(8,128)}, u32[]{:S(2)}) copy-start(f32[24,512]{1,0:T(8,128)} %copy-done.68) | copy-start | bytes 147460
  358.3 17.6 %copy-start.73 = (f32[24,512]{1,0:T(8,128)S(1)}, f32[24,512]{1,0:T(8,128)}, u32[]{:S(2)}) copy-start(f32[24,512]{1,0:T(8,128)} %get-tuple-element.122) | copy-start | bytes 147460
  358.4 17.6 %copy-start.74 = (f32[24,512]{1,0:T(8,128)S(1)}, f32[24,512]{1,0:T(8,128)}, u32[]{:S(2)}) copy-start(f32[24,512]{1,0:T(8,128)} %get-tuple-element.126) | copy-start | bytes 147460
  358.4 17.6 %copy-start.81 = (f32[24,512]{1,0:T(8,128)S(1)}, f32[24,512]{1,0:T(8,128)}, u32[]{:S(2)}) copy-start(f32[24,512]{1,0:T(8,128)} %copy-done.80) | copy-start | bytes 147460
  358.4 18.3 %copy-start.93 = (f32[10]{0:T(128)S(1)}, f32[10]{0:T(128)}, u32[]{:S(2)}) copy-start(f32[10]{0:T(128)} %copy-done.88) | copy-start | bytes 124
  384.8 7.5 %collective-permute-start.29 = (f32[10,1024]{1,0:T(8,128)S(1)}, f32[10,1024]{1,0:T(8,128)S(1)}, u32[]{:S(2)}, u32[]{:S(2)}) collective-permute-start(f32[10,1024]{1,0:T(8,128)S(1)} %bitcast.239), channel_id=1, source_target_pairs={{4,0},{8,4},{12,8},{16,12},{20,16},{24,20},{28,24},{5,1},{9,5},{13... | collective-permute-start | bytes 122888 | tf_op jit(solution)/shard_map/ppermute | solution.py:30
  394.6 5.8 collective-permute-start.30
  400.6 4.6 collective-permute-start.32
  401.9 4.7 collective-permute-start.31
  438.6 7.4 %collective-permute-start.33 = (f32[10,1024]{1,0:T(8,128)S(1)}, f32[10,1024]{1,0:T(8,128)S(1)}, u32[]{:S(2)}, u32[]{:S(2)}) collective-permute-start(f32[10,1024]{1,0:T(8,128)S(1)} %bitcast.241), channel_id=1, source_target_pairs={{4,0},{8,4},{12,8},{16,12},{20,16},{24,20},{28,24},{5,1},{9,5},{13... | collective-permute-start | bytes 122888 | tf_op jit(solution)/shard_map/ppermute | solution.py:30
  446.2 17.1 %slice-start.16 = ((s8[8388608]{0:T(1024)(128)(4,1)}), s8[4194304]{0:T(1024)(128)(4,1)S(1)}, s32[]{:S(2)}) async-start(s8[8388608]{0:T(1024)(128)(4,1)} %bitcast.222), calls=%async_computation.16 | async-start | bytes 8388608
  448.2 12.7 %copy-start.4 = (f32[24,8,1024]{2,0,1:T(8,128)}, f32[24,8,1024]{2,0,1:T(8,128)S(1)}, u32[]{:S(2)}) copy-start(f32[24,8,1024]{2,0,1:T(8,128)S(1)} %get-tuple-element.55) | copy-start | bytes 2359300
  448.3 5.8 collective-permute-start.34
  454.3 4.6 collective-permute-start.36
  455.9 4.5 collective-permute-start.35
  463.3 17.5 %copy-start.71 = (f32[24,512]{1,0:T(8,128)S(1)}, f32[24,512]{1,0:T(8,128)}, u32[]{:S(2)}) copy-start(f32[24,512]{1,0:T(8,128)} %copy-done.70) | copy-start | bytes 147460
  463.3 17.5 %copy-start.75 = (f32[24,512]{1,0:T(8,128)S(1)}, f32[24,512]{1,0:T(8,128)}, u32[]{:S(2)}) copy-start(f32[24,512]{1,0:T(8,128)} %get-tuple-element.126) | copy-start | bytes 147460
  463.3 17.5 %copy-start.83 = (f32[24,512]{1,0:T(8,128)S(1)}, f32[24,512]{1,0:T(8,128)}, u32[]{:S(2)}) copy-start(f32[24,512]{1,0:T(8,128)} %copy-done.82) | copy-start | bytes 147460
  463.3 17.5 %copy-start.86 = (f32[24,512]{1,0:T(8,128)S(1)}, f32[24,512]{1,0:T(8,128)}, u32[]{:S(2)}) copy-start(f32[24,512]{1,0:T(8,128)} %get-tuple-element.132) | copy-start | bytes 147460
  463.3 18.1 %copy-start.94 = (f32[10]{0:T(128)S(1)}, f32[10]{0:T(128)}, u32[]{:S(2)}) copy-start(f32[10]{0:T(128)} %copy-done.88) | copy-start | bytes 124
  489.6 7.5 %collective-permute-start.37 = (f32[10,1024]{1,0:T(8,128)S(1)}, f32[10,1024]{1,0:T(8,128)S(1)}, u32[]{:S(2)}, u32[]{:S(2)}) collective-permute-start(f32[10,1024]{1,0:T(8,128)S(1)} %bitcast.243), channel_id=1, source_target_pairs={{4,0},{8,4},{12,8},{16,12},{20,16},{24,20},{28,24},{5,1},{9,5},{13... | collective-permute-start | bytes 122888 | tf_op jit(solution)/shard_map/ppermute | solution.py:30
  497.3 17.1 %slice-start.18 = ((s8[8388608]{0:T(1024)(128)(4,1)}), s8[4194304]{0:T(1024)(128)(4,1)S(1)}, s32[]{:S(2)}) async-start(s8[8388608]{0:T(1024)(128)(4,1)} %bitcast.224), calls=%async_computation.18 | async-start | bytes 8388608
  499.4 5.8 collective-permute-start.38
  505.4 4.6 collective-permute-start.40
  506.9 4.5 collective-permute-start.39
  516.2 20.8 %copy-start.95 = (f32[10]{0:T(128)S(1)}, f32[10]{0:T(128)}, u32[]{:S(2)}) copy-start(f32[10]{0:T(128)} %copy-done.88) | copy-start | bytes 124
  545.5 10.6 %collective-permute-start.41 = (f32[10,1024]{1,0:T(8,128)S(1)}, f32[10,1024]{1,0:T(8,128)}, u32[]{:S(2)}, u32[]{:S(2)}) collective-permute-start(f32[10,1024]{1,0:T(8,128)S(1)} %bitcast.236), channel_id=1, source_target_pairs={{4,0},{8,4},{12,8},{16,12},{20,16},{24,20},{28,24},{5,1},{9,5},{13... | collective-permute-start | bytes 122888 | tf_op jit(solution)/shard_map/ppermute | solution.py:30
  (94 other events, 467.7 us)
where the time goes:
time: 635 us; the launch traced here: 625 us
  blocking collectives  207 us (33%)
  starting transfers between devices  120 us (19%)
  matrix products  104 us (16%)
  other arithmetic  67.4 us (11%)
  waiting for transfers between devices  61.4 us (10%)
  local copies, waits for them, and re-layouts  42 us (7%)
  between operations  23.2 us (4%)
    psum x10, blocking collectives, local(): pulled = lax.psum(partial_pull, 'state')  163 us
    dot_general x10, matrix products, apply_rows(): lax.dot_general(inputs_low, matrix, (((1,), (1,)), ((), ())), preferred_e...  73.3 us
    ppermute x20, starting transfers between devices, passed_along(): lax.ppermute(value, axis, [(source, source + steps) for source in range(l...  68.3 us
    ppermute x20, waiting for transfers between devices, passed_along(): lax.ppermute(value, axis, [(source, source + steps) for source in range(l...  50.4 us
    psum x1, blocking collectives, local(): totals = lax.psum((primal_square, gap_square), ('section', 'state'))  43.7 us
    ppermute x11, starting transfers between devices, with_halo(): lax.ppermute(lax.slice_in_dim(block, block.shape[dim] - width, None, axis...  36.6 us
    unnamed x245, local copies, waits for them, and re-layouts  26.6 us
    reduce_sum x10, other arithmetic, local(): primal_square = jnp.sum(primal * primal)  23.2 us
  transfers between devices with their start and end apart: 42, of which 28 were waited for; matrix products, arithmetic and copies ran while one was open for 5% of the time, Pallas kernels for 0%

commit v1 on v0

--- a/solution.py
+++ b/solution.py
@@ -83,7 +83,7 @@
         target = target_wide[:, 1:-1]
         target_low = target.astype(jnp.bfloat16).reshape(section_count, -1)
         partial_pull = jnp.dot(target_low, matrix, preferred_element_type=jnp.float32)
-        pulled = lax.psum(partial_pull, "state")
+        pulled = jnp.sum(lax.all_gather(partial_pull, "state"), axis=0)
         rhs_rows = pulled + penalty * (boxed - scaled)
         inputs = jnp.dot(rhs_rows, kkt_inverse, precision=lax.Precision.HIGHEST)
         inputs_low = inputs.astype(jnp.bfloat16)

time: 635 us -> 568 us (0.89)
  blocking collectives: 207 us -> 158 us
  other arithmetic: 67.4 us -> 51.9 us
  local copies, waits for them, and re-layouts: 42 us -> 29.2 us
    psum x10 -> x0, blocking collectives: 163 us -> none  [local(): pulled = lax.psum(partial_pull, 'state')]
    all_gather x0 -> x10, blocking collectives: none -> 115 us  [local(): pulled = jnp.sum(lax.all_gather(partial_pull, 'state'), axis=0)]
    add x6 -> x0, other arithmetic: 17.5 us -> none  [the longest x5 16.2 us: local(): target_wide = states_wide - moved_wide + duals_wide]
    unnamed x245 -> x237, local copies, waits for them, and re-layouts: 26.6 us -> 16.8 us
    reduce_sum x0 -> x10, other arithmetic: none -> 7.29 us  [local(): pulled = jnp.sum(lax.all_gather(partial_pull, 'state'), axis=0)]
  transfers between devices with their start and end apart: 42 -> 42, of which waited for: 28 -> 28; matrix products, arithmetic and copies ran while one was open for 5% -> 4% of each run, Pallas kernels for 0% -> 0%
where the time goes in v1:
time: 568 us; the launch traced here: 558 us
  blocking collectives  158 us (28%)
  starting transfers between devices  120 us (21%)
  matrix products  109 us (19%)
  waiting for transfers between devices  66 us (12%)
  other arithmetic  51.9 us (9%)
  local copies, waits for them, and re-layouts  29.2 us (5%)
  between operations  23.3 us (4%)
    all_gather x10, blocking collectives, local(): pulled = jnp.sum(lax.all_gather(partial_pull, 'state'), axis=0)  115 us
    dot_general x10, matrix products, apply_rows(): lax.dot_general(inputs_low, matrix, (((1,), (1,)), ((), ())), preferred_e...  78.7 us
    ppermute x20, starting transfers between devices, passed_along(): lax.ppermute(value, axis, [(source, source + steps) for source in range(l...  69.5 us
    ppermute x20, waiting for transfers between devices, passed_along(): lax.ppermute(value, axis, [(source, source + steps) for source in range(l...  53.5 us
    psum x1, blocking collectives, local(): totals = lax.psum((primal_square, gap_square), ('section', 'state'))  43.1 us
    ppermute x11, starting transfers between devices, with_halo(): lax.ppermute(lax.slice_in_dim(block, block.shape[dim] - width, None, axis...  36.7 us
    reduce_sum x10, other arithmetic, local(): primal_square = jnp.sum(primal * primal)  22.8 us
    unnamed x237, local copies, waits for them, and re-layouts  16.8 us
  transfers between devices with their start and end apart: 42, of which 28 were waited for; matrix products, arithmetic and copies ran while one was open for 4% of the time, Pallas kernels for 0%

profile of v1, /device:TPU:12, one launch (start us, length us, event | category | flops | bytes accessed | tf_op | source)
XLA Modules:
  0.0 557.9 jit_solution(11621624884877160638)
XLA Ops:
  0.7 3.6 collective-permute-start
  8.0 3.1 collective-permute-start.1
  14.1 4.0 collective-permute-start.3
  21.6 5.0 convolution_bitcast_fusion.9
  26.6 9.5 %all-gather = f32[96,512]{1,0:T(8,128)S(1)} all-gather(f32[24,512]{1,0:T(8,128)S(1)} %convolution_bitcast_fusion.9), channel_id=2, replica_groups=mesh['section'=8,'state'=4] {'state'}, dimensions={0}, use_global_device_ids=true | all-gather | bytes 245760 | tf_op jit(solution)/shard_map/all_gather | solution.py:86
  39.0 7.3 %constant_dynamic-update-slice_fusion.1 = bf16[10,1024,512]{2,1,0:T(8,128)(2,1)} fusion(bf16[10,1024,512]{2,1,0:T(8,128)(2,1)} %constant_dynamic-update-slice_fusion.2, bf16[8,1024,512]{2,1,0:T(8,128)(2,1)} %param.9), kind=kLoop, calls=%fused_computation.736 | loop fusion | bytes 16777216
  48.6 7.5 %subtract_multiply_fusion.9 = (f32[24,10,1024]{2,0,1:T(8,128)S(1)}, f32[24,10,1024]{2,0,1:T(8,128)S(1)}) fusion(f32[10]{0:T(128)S(1)} %or_select_fusion, f32[49,12,1024]{2,0,1:T(8,128)} %copy-done.48, f32[24,10,1024]{2,0,1:T(8,128)S(1)} %fusion.5, bf16[10,1024,512]{2,1,0:T(8,128)(2,1)} %constant_dynamic-update-slice_fusion, f32[24,512]{1,0:T(8,128)S(1)} %fusion.421), kind=kOutput, calls=%fused_computation.267 | convolution fusion | flops 252653568 | bytes 15450152 | tf_op jit(solution)/shard_map/dot_general | solution.py:47
  56.2 3.4 collective-permute-start.5
  59.7 3.7 collective-permute-done.5
  66.0 3.4 collective-permute-start.6
  81.1 11.2 %all-gather.1 = f32[96,512]{1,0:T(8,128)} all-gather(f32[24,512]{1,0:T(8,128)S(1)} %convolution_bitcast_fusion.8), channel_id=3, replica_groups=mesh['section'=8,'state'=4] {'state'}, dimensions={0}, use_global_device_ids=true | all-gather | bytes 245760 | tf_op jit(solution)/shard_map/all_gather | solution.py:86
  94.4 7.8 %subtract_multiply_fusion.8 = (f32[24,10,1024]{2,0,1:T(8,128)S(1)}, f32[24,10,1024]{2,0,1:T(8,128)S(1)}) fusion(f32[10]{0:T(128)} %copy-done.83, f32[49,12,1024]{2,0,1:T(8,128)} %copy-done.49, f32[24,10,1024]{2,0,1:T(8,128)} %copy-done.10, bf16[10,1024,512]{2,1,0:T(8,128)(2,1)} %constant_dynamic-update-slice_fusion, f32[24,512]{1,0:T(8,128)S(1)} %get-tuple-element.105), kind=kOutput, calls=%fused_computation.266 | convolution fusion | flops 252653568 | bytes 15450152 | tf_op jit(solution)/shard_map/dot_general | solution.py:47
  102.3 3.4 collective-permute-start.9
  105.9 3.7 collective-permute-done.9
  111.9 3.4 collective-permute-start.10
  119.2 3.3 collective-permute-start.11
  127.3 11.6 %all-gather.2 = f32[96,512]{1,0:T(8,128)S(1)} all-gather(f32[24,512]{1,0:T(8,128)S(1)} %convolution_bitcast_fusion.7), channel_id=4, replica_groups=mesh['section'=8,'state'=4] {'state'}, dimensions={0}, use_global_device_ids=true | all-gather | bytes 245760 | tf_op jit(solution)/shard_map/all_gather | solution.py:86
  139.6 7.8 %subtract_multiply_fusion.7 = (f32[24,10,1024]{2,0,1:T(8,128)S(1)}, f32[24,10,1024]{2,0,1:T(8,128)S(1)}) fusion(f32[10]{0:T(128)S(1)} %copy-done.84, f32[49,12,1024]{2,0,1:T(8,128)} %copy-done.53, f32[24,10,1024]{2,0,1:T(8,128)} %copy-done.18, bf16[10,1024,512]{2,1,0:T(8,128)(2,1)} %constant_dynamic-update-slice_fusion, f32[24,512]{1,0:T(8,128)S(1)} %fusion.297), kind=kOutput, calls=%fused_computation.265 | convolution fusion | flops 252653568 | bytes 15450152 | tf_op jit(solution)/shard_map/dot_general | solution.py:47
  147.4 3.4 collective-permute-start.13
  151.0 3.7 collective-permute-done.13
  156.9 3.6 collective-permute-start.14
  164.2 3.3 collective-permute-start.15
  172.2 12.0 %all-gather.3 = f32[96,512]{1,0:T(8,128)} all-gather(f32[24,512]{1,0:T(8,128)S(1)} %convolution_bitcast_fusion.6), channel_id=5, replica_groups=mesh['section'=8,'state'=4] {'state'}, dimensions={0}, use_global_device_ids=true | all-gather | bytes 245760 | tf_op jit(solution)/shard_map/all_gather | solution.py:86
  187.9 7.8 %subtract_multiply_fusion.6 = (f32[24,10,1024]{2,0,1:T(8,128)S(1)}, f32[24,10,1024]{2,0,1:T(8,128)S(1)}) fusion(f32[10]{0:T(128)} %copy-done.83, f32[49,12,1024]{2,0,1:T(8,128)} %copy-done.50, f32[24,10,1024]{2,0,1:T(8,128)} %copy-done.12, bf16[10,1024,512]{2,1,0:T(8,128)(2,1)} %constant_dynamic-update-slice_fusion, f32[24,512]{1,0:T(8,128)S(1)} %get-tuple-element.111), kind=kOutput, calls=%fused_computation.264 | convolution fusion | flops 252653568 | bytes 15450152 | tf_op jit(solution)/shard_map/dot_general | solution.py:47
  195.8 3.4 collective-permute-start.17
  199.4 3.7 collective-permute-done.17
  205.3 3.4 collective-permute-start.18
  212.6 3.3 collective-permute-start.19
  220.7 11.8 %all-gather.4 = f32[96,512]{1,0:T(8,128)S(1)} all-gather(f32[24,512]{1,0:T(8,128)S(1)} %convolution_bitcast_fusion.5), channel_id=6, replica_groups=mesh['section'=8,'state'=4] {'state'}, dimensions={0}, use_global_device_ids=true | all-gather | bytes 245760 | tf_op jit(solution)/shard_map/all_gather | solution.py:86
  233.2 7.8 %subtract_multiply_fusion.5 = (f32[24,10,1024]{2,0,1:T(8,128)S(1)}, f32[24,10,1024]{2,0,1:T(8,128)S(1)}) fusion(f32[10]{0:T(128)S(1)} %copy-done.85, f32[49,12,1024]{2,0,1:T(8,128)} %copy-done.54, f32[24,10,1024]{2,0,1:T(8,128)} %copy-done.20, bf16[10,1024,512]{2,1,0:T(8,128)(2,1)} %constant_dynamic-update-slice_fusion, f32[24,512]{1,0:T(8,128)S(1)} %fusion.289), kind=kOutput, calls=%fused_computation.263 | convolution fusion | flops 252653568 | bytes 15450152 | tf_op jit(solution)/shard_map/dot_general | solution.py:47
  241.1 3.4 collective-permute-start.21
  244.7 3.7 collective-permute-done.21
  250.7 3.4 collective-permute-start.22
  258.0 3.3 collective-permute-start.23
  266.0 12.0 %all-gather.5 = f32[96,512]{1,0:T(8,128)} all-gather(f32[24,512]{1,0:T(8,128)S(1)} %convolution_bitcast_fusion.4), channel_id=7, replica_groups=mesh['section'=8,'state'=4] {'state'}, dimensions={0}, use_global_device_ids=true | all-gather | bytes 245760 | tf_op jit(solution)/shard_map/all_gather | solution.py:86
  281.7 7.8 %subtract_multiply_fusion.4 = (f32[24,10,1024]{2,0,1:T(8,128)S(1)}, f32[24,10,1024]{2,0,1:T(8,128)S(1)}) fusion(f32[10]{0:T(128)} %copy-done.83, f32[49,12,1024]{2,0,1:T(8,128)} %copy-done.51, f32[24,10,1024]{2,0,1:T(8,128)} %copy-done.14, bf16[10,1024,512]{2,1,0:T(8,128)(2,1)} %constant_dynamic-update-slice_fusion, f32[24,512]{1,0:T(8,128)S(1)} %get-tuple-element.117), kind=kOutput, calls=%fused_computation.262 | convolution fusion | flops 252653568 | bytes 15450152 | tf_op jit(solution)/shard_map/dot_general | solution.py:47
  289.6 3.4 collective-permute-start.25
  293.2 3.7 collective-permute-done.25
  299.2 3.8 collective-permute-start.26
  306.5 3.3 collective-permute-start.27
  314.6 11.6 %all-gather.6 = f32[96,512]{1,0:T(8,128)S(1)} all-gather(f32[24,512]{1,0:T(8,128)S(1)} %convolution_bitcast_fusion.3), channel_id=8, replica_groups=mesh['section'=8,'state'=4] {'state'}, dimensions={0}, use_global_device_ids=true | all-gather | bytes 245760 | tf_op jit(solution)/shard_map/all_gather | solution.py:86
  326.9 7.8 %subtract_multiply_fusion.3 = (f32[24,10,1024]{2,0,1:T(8,128)S(1)}, f32[24,10,1024]{2,0,1:T(8,128)S(1)}) fusion(f32[10]{0:T(128)S(1)} %copy-done.86, f32[49,12,1024]{2,0,1:T(8,128)} %copy-done.55, f32[24,10,1024]{2,0,1:T(8,128)} %copy-done.22, bf16[10,1024,512]{2,1,0:T(8,128)(2,1)} %constant_dynamic-update-slice_fusion, f32[24,512]{1,0:T(8,128)S(1)} %fusion.281), kind=kOutput, calls=%fused_computation.261 | convolution fusion | flops 252653568 | bytes 15450152 | tf_op jit(solution)/shard_map/dot_general | solution.py:47
  334.7 3.4 collective-permute-start.29
  338.3 3.7 collective-permute-done.29
  344.3 3.4 collective-permute-start.30
  351.6 3.3 collective-permute-start.31
  359.6 12.2 %all-gather.7 = f32[96,512]{1,0:T(8,128)} all-gather(f32[24,512]{1,0:T(8,128)S(1)} %convolution_bitcast_fusion.2), channel_id=9, replica_groups=mesh['section'=8,'state'=4] {'state'}, dimensions={0}, use_global_device_ids=true | all-gather | bytes 245760 | tf_op jit(solution)/shard_map/all_gather | solution.py:86
  375.5 7.8 %subtract_multiply_fusion.2 = (f32[24,10,1024]{2,0,1:T(8,128)S(1)}, f32[24,10,1024]{2,0,1:T(8,128)S(1)}) fusion(f32[10]{0:T(128)} %copy-done.83, f32[49,12,1024]{2,0,1:T(8,128)} %copy-done.52, f32[24,10,1024]{2,0,1:T(8,128)} %copy-done.16, bf16[10,1024,512]{2,1,0:T(8,128)(2,1)} %constant_dynamic-update-slice_fusion, f32[24,512]{1,0:T(8,128)S(1)} %get-tuple-element.123), kind=kOutput, calls=%fused_computation.260 | convolution fusion | flops 252653568 | bytes 15450152 | tf_op jit(solution)/shard_map/dot_general | solution.py:47
  383.4 3.4 collective-permute-start.33
  387.0 3.7 collective-permute-done.33
  392.9 3.4 collective-permute-start.34
  400.2 3.3 collective-permute-start.35
  408.3 11.6 %all-gather.8 = f32[96,512]{1,0:T(8,128)S(1)} all-gather(f32[24,512]{1,0:T(8,128)S(1)} %convolution_bitcast_fusion.1), channel_id=10, replica_groups=mesh['section'=8,'state'=4] {'state'}, dimensions={0}, use_global_device_ids=true | all-gather | bytes 245760 | tf_op jit(solution)/shard_map/all_gather | solution.py:86
  420.6 7.8 %subtract_multiply_fusion.1 = (f32[24,10,1024]{2,0,1:T(8,128)S(1)}, f32[24,10,1024]{2,0,1:T(8,128)S(1)}) fusion(f32[10]{0:T(128)S(1)} %copy-done.87, f32[49,12,1024]{2,0,1:T(8,128)} %copy-done.56, f32[24,10,1024]{2,0,1:T(8,128)} %copy-done.24, bf16[10,1024,512]{2,1,0:T(8,128)(2,1)} %constant_dynamic-update-slice_fusion, f32[24,512]{1,0:T(8,128)S(1)} %fusion.273), kind=kOutput, calls=%fused_computation.259 | convolution fusion | flops 252653568 | bytes 15450152 | tf_op jit(solution)/shard_map/dot_general | solution.py:47
  428.5 3.4 collective-permute-start.37
  432.1 3.7 collective-permute-done.37
  438.1 3.6 collective-permute-start.38
  445.4 3.3 collective-permute-start.39
  453.4 12.0 %all-gather.9 = f32[96,512]{1,0:T(8,128)} all-gather(f32[24,512]{1,0:T(8,128)S(1)} %convolution_bitcast_fusion), channel_id=11, replica_groups=mesh['section'=8,'state'=4] {'state'}, dimensions={0}, use_global_device_ids=true | all-gather | bytes 245760 | tf_op jit(solution)/shard_map/all_gather | solution.py:86
  466.9 3.1 multiply_reduce_fusion.12
  470.0 8.8 %subtract_multiply_fusion = (f32[24,10,1024]{2,0,1:T(8,128)S(1)}, f32[24,10,1024]{2,0,1:T(8,128)}) fusion(f32[10]{0:T(128)S(1)} %copy-done.88, f32[49,12,1024]{2,0,1:T(8,128)} %copy-done.57, f32[24,10,1024]{2,0,1:T(8,128)} %copy-done.26, bf16[10,1024,512]{2,1,0:T(8,128)(2,1)} %constant_dynamic-update-slice_fusion, bf16[24,512]{1,0:T(8,128)(2,1)S(1)} %get-tuple-element.128), kind=kOutput, calls=%fused_computation.258 | convolution fusion | flops 252641280 | bytes 15425576 | tf_op jit(solution)/shard_map/dot_general | solution.py:47
  478.8 3.3 collective-permute-start.41
  491.8 4.1 multiply_reduce_fusion
  498.8 43.1 %all-reduce.61 = (f32[]{:T(128)}, f32[]{:T(128)}, f32[]{:T(128)}, f32[]{:T(128)}, f32[]{:T(128)}, /*index=5*/f32[]{:T(128)}, f32[]{:T(128)}, f32[]{:T(128)}, f32...) all-reduce(f32[]{:T(128)S(6)} %div.131, ...), channel_id=1, replica_groups=mesh['section'=8,'state'=4] {'section','state'}, use_global_device_ids=true, to_apply=%region_13.14 | all-reduce | flops 20 | bytes 160 | tf_op jit(solution)/shard_map/psum | solution.py:111
  (473 shorter events, 142.0 us)
Async XLA Ops:
  0.6 35.4 %copy-start = (f32[512,512]{1,0:T(8,128)S(1)}, f32[512,512]{1,0:T(8,128)}, u32[]{:S(2)}) copy-start(f32[512,512]{1,0:T(8,128)} %param.10) | copy-start | bytes 3145732
  0.7 5.9 %collective-permute-start = (f32[8,1024]{1,0:T(8,128)S(1)}, f32[8,1024]{1,0:T(8,128)S(1)}, u32[]{:S(2)}, u32[]{:S(2)}) collective-permute-start(f32[8,1024]{1,0:T(8,128)S(1)} %squeeze.60), channel_id=1, source_target_pairs={{0,4},{4,8},{8,12},{12,16},{16,20},{20,24},{24,28},{1,5},{5,9},{9,... | collective-permute-start | bytes 98312 | tf_op jit(solution)/shard_map/ppermute | solution.py:30
  6.7 12.9 %collective-permute-start.2 = (f32[49,2,1024]{2,0,1:T(8,128)S(1)}, f32[49,2,1024]{2,0,1:T(8,128)S(1)}, u32[]{:S(2)}, u32[]{:S(2)}) collective-permute-start(f32[49,2,1024]{2,0,1:T(8,128)S(1)} %get-tuple-element.99), channel_id=1, source_target_pairs={{1,0},{2,1},{3,2},{5,4},{6,5},{7,6},{9,8},{10,9},{11,10},{13,12},{... | collective-permute-start | bytes 1204232 | tf_op jit(solution)/shard_map/ppermute | solution.py:22
  8.0 11.6 %collective-permute-start.1 = (f32[49,2,1024]{2,0,1:T(8,128)S(1)}, f32[49,2,1024]{2,0,1:T(8,128)S(1)}, u32[]{:S(2)}, u32[]{:S(2)}) collective-permute-start(f32[49,2,1024]{2,0,1:T(8,128)S(1)} %get-tuple-element.98), channel_id=1, source_target_pairs={{0,1},{1,2},{2,3},{4,5},{5,6},{6,7},{8,9},{9,10},{10,11},{12,13},{... | collective-permute-start | bytes 1204232 | tf_op jit(solution)/shard_map/ppermute | solution.py:19
  14.1 22.6 %collective-permute-start.3 = (bf16[1,1024,512]{2,1,0:T(8,128)(2,1)}, bf16[1,1024,512]{2,1,0:T(8,128)(2,1)}, u32[]{:S(2)}, u32[]{:S(2)}) collective-permute-start(bf16[1,1024,512]{2,1,0:T(8,128)(2,1)} %get-tuple-element.77), channel_id=1, source_target_pairs={{0,1},{1,2},{2,3},{4,5},{5,6},{6,7},{8,9},{9,10},{10,11},{12,13},{... | collective-permute-start | bytes 3145736 | tf_op jit(solution)/shard_map/ppermute | solution.py:19
  18.1 28.2 %collective-permute-start.4 = (bf16[1,1024,512]{2,1,0:T(8,128)(2,1)}, bf16[1,1024,512]{2,1,0:T(8,128)(2,1)}, u32[]{:S(2)}, u32[]{:S(2)}) collective-permute-start(bf16[1,1024,512]{2,1,0:T(8,128)(2,1)} %get-tuple-element.76), channel_id=1, source_target_pairs={{1,0},{2,1},{3,2},{5,4},{6,5},{7,6},{9,8},{10,9},{11,10},{13,12},{... | collective-permute-start | bytes 3145736 | tf_op jit(solution)/shard_map/ppermute | solution.py:22
  19.4 29.1 %copy-start.83 = (f32[10]{0:T(128)}, f32[10]{0:T(128)S(1)}, u32[]{:S(2)}) copy-start(f32[10]{0:T(128)S(1)} %or_select_fusion) | copy-start | bytes 124
  21.6 27.0 %copy-start.46 = (f32[24,10,1024]{2,0,1:T(8,128)}, f32[24,10,1024]{2,0,1:T(8,128)S(1)}, u32[]{:S(2)}) copy-start(f32[24,10,1024]{2,0,1:T(8,128)S(1)} %fusion.5) | copy-start | bytes 2949124
  56.2 7.3 %collective-permute-start.5 = (f32[10,1024]{1,0:T(8,128)S(1)}, f32[10,1024]{1,0:T(8,128)S(1)}, u32[]{:S(2)}, u32[]{:S(2)}) collective-permute-start(f32[10,1024]{1,0:T(8,128)S(1)} %bitcast.265), channel_id=1, source_target_pairs={{4,0},{8,4},{12,8},{16,12},{20,16},{24,20},{28,24},{5,1},{9,5},{13... | collective-permute-start | bytes 122888 | tf_op jit(solution)/shard_map/ppermute | solution.py:30
  63.6 16.2 %slice-start = ((s8[8388608]{0:T(1024)(128)(4,1)}), s8[4194304]{0:T(1024)(128)(4,1)S(1)}, s32[]{:S(2)}) async-start(s8[8388608]{0:T(1024)(128)(4,1)} %bitcast.236), calls=%async_computation | async-start | bytes 8388608
  66.0 5.8 %collective-permute-start.6 = (f32[8,1024]{1,0:T(8,128)S(1)}, f32[8,1024]{1,0:T(8,128)S(1)}, u32[]{:S(2)}, u32[]{:S(2)}) collective-permute-start(f32[8,1024]{1,0:T(8,128)S(1)} %bitcast.291), channel_id=1, source_target_pairs={{0,4},{4,8},{8,12},{12,16},{16,20},{20,24},{24,28},{1,5},{5,9},{9,... | collective-permute-start | bytes 98312 | tf_op jit(solution)/shard_map/ppermute | solution.py:30
  72.0 4.4 collective-permute-start.8
  73.3 4.5 collective-permute-start.7
  102.3 7.3 %collective-permute-start.9 = (f32[10,1024]{1,0:T(8,128)S(1)}, f32[10,1024]{1,0:T(8,128)S(1)}, u32[]{:S(2)}, u32[]{:S(2)}) collective-permute-start(f32[10,1024]{1,0:T(8,128)S(1)} %bitcast.267), channel_id=1, source_target_pairs={{4,0},{8,4},{12,8},{16,12},{20,16},{24,20},{28,24},{5,1},{9,5},{13... | collective-permute-start | bytes 122888 | tf_op jit(solution)/shard_map/ppermute | solution.py:30
  111.9 5.8 %collective-permute-start.10 = (f32[8,1024]{1,0:T(8,128)S(1)}, f32[8,1024]{1,0:T(8,128)S(1)}, u32[]{:S(2)}, u32[]{:S(2)}) collective-permute-start(f32[8,1024]{1,0:T(8,128)S(1)} %bitcast.283), channel_id=1, source_target_pairs={{0,4},{4,8},{8,12},{12,16},{16,20},{20,24},{24,28},{1,5},{5,9},{9,... | collective-permute-start | bytes 98312 | tf_op jit(solution)/shard_map/ppermute | solution.py:30
  117.9 4.6 collective-permute-start.12
  119.2 4.7 collective-permute-start.11
  126.0 12.9 %copy-start.61 = (f32[24,512]{1,0:T(8,128)S(1)}, f32[24,512]{1,0:T(8,128)}, u32[]{:S(2)}) copy-start(f32[24,512]{1,0:T(8,128)} %get-tuple-element.104) | copy-start | bytes 147460
  126.0 12.8 %copy-start.72 = (f32[24,512]{1,0:T(8,128)S(1)}, f32[24,512]{1,0:T(8,128)}, u32[]{:S(2)}) copy-start(f32[24,512]{1,0:T(8,128)} %copy-done.71) | copy-start | bytes 147460
  126.1 13.5 %copy-start.84 = (f32[10]{0:T(128)S(1)}, f32[10]{0:T(128)}, u32[]{:S(2)}) copy-start(f32[10]{0:T(128)} %copy-done.83) | copy-start | bytes 124
  147.4 7.3 %collective-permute-start.13 = (f32[10,1024]{1,0:T(8,128)S(1)}, f32[10,1024]{1,0:T(8,128)S(1)}, u32[]{:S(2)}, u32[]{:S(2)}) collective-permute-start(f32[10,1024]{1,0:T(8,128)S(1)} %bitcast.269), channel_id=1, source_target_pairs={{4,0},{8,4},{12,8},{16,12},{20,16},{24,20},{28,24},{5,1},{9,5},{13... | collective-permute-start | bytes 122888 | tf_op jit(solution)/shard_map/ppermute | solution.py:30
  156.9 5.8 %collective-permute-start.14 = (f32[8,1024]{1,0:T(8,128)S(1)}, f32[8,1024]{1,0:T(8,128)S(1)}, u32[]{:S(2)}, u32[]{:S(2)}) collective-permute-start(f32[8,1024]{1,0:T(8,128)S(1)} %bitcast.284), channel_id=1, source_target_pairs={{0,4},{4,8},{8,12},{12,16},{16,20},{20,24},{24,28},{1,5},{5,9},{9,... | collective-permute-start | bytes 98312 | tf_op jit(solution)/shard_map/ppermute | solution.py:30
  162.9 4.6 collective-permute-start.16
  164.2 4.7 collective-permute-start.15
  195.8 7.3 %collective-permute-start.17 = (f32[10,1024]{1,0:T(8,128)S(1)}, f32[10,1024]{1,0:T(8,128)S(1)}, u32[]{:S(2)}, u32[]{:S(2)}) collective-permute-start(f32[10,1024]{1,0:T(8,128)S(1)} %bitcast.271), channel_id=1, source_target_pairs={{4,0},{8,4},{12,8},{16,12},{20,16},{24,20},{28,24},{5,1},{9,5},{13... | collective-permute-start | bytes 122888 | tf_op jit(solution)/shard_map/ppermute | solution.py:30
  205.3 5.8 %collective-permute-start.18 = (f32[8,1024]{1,0:T(8,128)S(1)}, f32[8,1024]{1,0:T(8,128)S(1)}, u32[]{:S(2)}, u32[]{:S(2)}) collective-permute-start(f32[8,1024]{1,0:T(8,128)S(1)} %bitcast.285), channel_id=1, source_target_pairs={{0,4},{4,8},{8,12},{12,16},{16,20},{20,24},{24,28},{1,5},{5,9},{9,... | collective-permute-start | bytes 98312 | tf_op jit(solution)/shard_map/ppermute | solution.py:30
  211.3 4.6 collective-permute-start.20
  212.6 4.7 collective-permute-start.19
  219.4 13.1 %copy-start.62 = (f32[24,512]{1,0:T(8,128)S(1)}, f32[24,512]{1,0:T(8,128)}, u32[]{:S(2)}) copy-start(f32[24,512]{1,0:T(8,128)} %get-tuple-element.104) | copy-start | bytes 147460
  219.4 13.1 %copy-start.67 = (f32[24,512]{1,0:T(8,128)S(1)}, f32[24,512]{1,0:T(8,128)}, u32[]{:S(2)}) copy-start(f32[24,512]{1,0:T(8,128)} %get-tuple-element.110) | copy-start | bytes 147460
  219.5 13.1 %copy-start.74 = (f32[24,512]{1,0:T(8,128)S(1)}, f32[24,512]{1,0:T(8,128)}, u32[]{:S(2)}) copy-start(f32[24,512]{1,0:T(8,128)} %copy-done.73) | copy-start | bytes 147460
  219.5 13.7 %copy-start.85 = (f32[10]{0:T(128)S(1)}, f32[10]{0:T(128)}, u32[]{:S(2)}) copy-start(f32[10]{0:T(128)} %copy-done.83) | copy-start | bytes 124
  241.1 7.3 %collective-permute-start.21 = (f32[10,1024]{1,0:T(8,128)S(1)}, f32[10,1024]{1,0:T(8,128)S(1)}, u32[]{:S(2)}, u32[]{:S(2)}) collective-permute-start(f32[10,1024]{1,0:T(8,128)S(1)} %bitcast.273), channel_id=1, source_target_pairs={{4,0},{8,4},{12,8},{16,12},{20,16},{24,20},{28,24},{5,1},{9,5},{13... | collective-permute-start | bytes 122888 | tf_op jit(solution)/shard_map/ppermute | solution.py:30
  250.7 5.8 %collective-permute-start.22 = (f32[8,1024]{1,0:T(8,128)S(1)}, f32[8,1024]{1,0:T(8,128)S(1)}, u32[]{:S(2)}, u32[]{:S(2)}) collective-permute-start(f32[8,1024]{1,0:T(8,128)S(1)} %bitcast.286), channel_id=1, source_target_pairs={{0,4},{4,8},{8,12},{12,16},{16,20},{20,24},{24,28},{1,5},{5,9},{9,... | collective-permute-start | bytes 98312 | tf_op jit(solution)/shard_map/ppermute | solution.py:30
  256.7 4.6 collective-permute-start.24
  258.0 4.7 collective-permute-start.23
  289.6 7.3 %collective-permute-start.25 = (f32[10,1024]{1,0:T(8,128)S(1)}, f32[10,1024]{1,0:T(8,128)S(1)}, u32[]{:S(2)}, u32[]{:S(2)}) collective-permute-start(f32[10,1024]{1,0:T(8,128)S(1)} %bitcast.275), channel_id=1, source_target_pairs={{4,0},{8,4},{12,8},{16,12},{20,16},{24,20},{28,24},{5,1},{9,5},{13... | collective-permute-start | bytes 122888 | tf_op jit(solution)/shard_map/ppermute | solution.py:30
  299.2 5.8 %collective-permute-start.26 = (f32[8,1024]{1,0:T(8,128)S(1)}, f32[8,1024]{1,0:T(8,128)S(1)}, u32[]{:S(2)}, u32[]{:S(2)}) collective-permute-start(f32[8,1024]{1,0:T(8,128)S(1)} %bitcast.287), channel_id=1, source_target_pairs={{0,4},{4,8},{8,12},{12,16},{16,20},{20,24},{24,28},{1,5},{5,9},{9,... | collective-permute-start | bytes 98312 | tf_op jit(solution)/shard_map/ppermute | solution.py:30
  305.2 4.6 collective-permute-start.28
  306.5 4.7 collective-permute-start.27
  313.3 12.9 %copy-start.64 = (f32[24,512]{1,0:T(8,128)S(1)}, f32[24,512]{1,0:T(8,128)}, u32[]{:S(2)}) copy-start(f32[24,512]{1,0:T(8,128)} %copy-done.63) | copy-start | bytes 147460
  313.3 12.9 %copy-start.68 = (f32[24,512]{1,0:T(8,128)S(1)}, f32[24,512]{1,0:T(8,128)}, u32[]{:S(2)}) copy-start(f32[24,512]{1,0:T(8,128)} %get-tuple-element.110) | copy-start | bytes 147460
  313.3 12.9 %copy-start.69 = (f32[24,512]{1,0:T(8,128)S(1)}, f32[24,512]{1,0:T(8,128)}, u32[]{:S(2)}) copy-start(f32[24,512]{1,0:T(8,128)} %get-tuple-element.116) | copy-start | bytes 147460
  313.3 12.9 %copy-start.76 = (f32[24,512]{1,0:T(8,128)S(1)}, f32[24,512]{1,0:T(8,128)}, u32[]{:S(2)}) copy-start(f32[24,512]{1,0:T(8,128)} %copy-done.75) | copy-start | bytes 147460
  313.3 13.5 %copy-start.86 = (f32[10]{0:T(128)S(1)}, f32[10]{0:T(128)}, u32[]{:S(2)}) copy-start(f32[10]{0:T(128)} %copy-done.83) | copy-start | bytes 124
  334.7 7.3 %collective-permute-start.29 = (f32[10,1024]{1,0:T(8,128)S(1)}, f32[10,1024]{1,0:T(8,128)S(1)}, u32[]{:S(2)}, u32[]{:S(2)}) collective-permute-start(f32[10,1024]{1,0:T(8,128)S(1)} %bitcast.277), channel_id=1, source_target_pairs={{4,0},{8,4},{12,8},{16,12},{20,16},{24,20},{28,24},{5,1},{9,5},{13... | collective-permute-start | bytes 122888 | tf_op jit(solution)/shard_map/ppermute | solution.py:30
  344.3 5.8 %collective-permute-start.30 = (f32[8,1024]{1,0:T(8,128)S(1)}, f32[8,1024]{1,0:T(8,128)S(1)}, u32[]{:S(2)}, u32[]{:S(2)}) collective-permute-start(f32[8,1024]{1,0:T(8,128)S(1)} %bitcast.288), channel_id=1, source_target_pairs={{0,4},{4,8},{8,12},{12,16},{16,20},{20,24},{24,28},{1,5},{5,9},{9,... | collective-permute-start | bytes 98312 | tf_op jit(solution)/shard_map/ppermute | solution.py:30
  350.3 4.6 collective-permute-start.32
  351.6 4.7 collective-permute-start.31
  383.4 7.3 %collective-permute-start.33 = (f32[10,1024]{1,0:T(8,128)S(1)}, f32[10,1024]{1,0:T(8,128)S(1)}, u32[]{:S(2)}, u32[]{:S(2)}) collective-permute-start(f32[10,1024]{1,0:T(8,128)S(1)} %bitcast.279), channel_id=1, source_target_pairs={{4,0},{8,4},{12,8},{16,12},{20,16},{24,20},{28,24},{5,1},{9,5},{13... | collective-permute-start | bytes 122888 | tf_op jit(solution)/shard_map/ppermute | solution.py:30
  392.9 5.8 %collective-permute-start.34 = (f32[8,1024]{1,0:T(8,128)S(1)}, f32[8,1024]{1,0:T(8,128)S(1)}, u32[]{:S(2)}, u32[]{:S(2)}) collective-permute-start(f32[8,1024]{1,0:T(8,128)S(1)} %bitcast.289), channel_id=1, source_target_pairs={{0,4},{4,8},{8,12},{12,16},{16,20},{20,24},{24,28},{1,5},{5,9},{9,... | collective-permute-start | bytes 98312 | tf_op jit(solution)/shard_map/ppermute | solution.py:30
  398.9 4.6 collective-permute-start.36
  400.2 4.7 collective-permute-start.35
  407.0 12.9 %copy-start.66 = (f32[24,512]{1,0:T(8,128)S(1)}, f32[24,512]{1,0:T(8,128)}, u32[]{:S(2)}) copy-start(f32[24,512]{1,0:T(8,128)} %copy-done.65) | copy-start | bytes 147460
  407.1 12.9 %copy-start.70 = (f32[24,512]{1,0:T(8,128)S(1)}, f32[24,512]{1,0:T(8,128)}, u32[]{:S(2)}) copy-start(f32[24,512]{1,0:T(8,128)} %get-tuple-element.116) | copy-start | bytes 147460
  407.1 12.9 %copy-start.78 = (f32[24,512]{1,0:T(8,128)S(1)}, f32[24,512]{1,0:T(8,128)}, u32[]{:S(2)}) copy-start(f32[24,512]{1,0:T(8,128)} %copy-done.77) | copy-start | bytes 147460
  407.1 12.9 %copy-start.81 = (f32[24,512]{1,0:T(8,128)S(1)}, f32[24,512]{1,0:T(8,128)}, u32[]{:S(2)}) copy-start(f32[24,512]{1,0:T(8,128)} %get-tuple-element.122) | copy-start | bytes 147460
  407.1 13.5 %copy-start.87 = (f32[10]{0:T(128)S(1)}, f32[10]{0:T(128)}, u32[]{:S(2)}) copy-start(f32[10]{0:T(128)} %copy-done.83) | copy-start | bytes 124
  428.5 7.3 %collective-permute-start.37 = (f32[10,1024]{1,0:T(8,128)S(1)}, f32[10,1024]{1,0:T(8,128)S(1)}, u32[]{:S(2)}, u32[]{:S(2)}) collective-permute-start(f32[10,1024]{1,0:T(8,128)S(1)} %bitcast.281), channel_id=1, source_target_pairs={{4,0},{8,4},{12,8},{16,12},{20,16},{24,20},{28,24},{5,1},{9,5},{13... | collective-permute-start | bytes 122888 | tf_op jit(solution)/shard_map/ppermute | solution.py:30
  438.1 5.8 %collective-permute-start.38 = (f32[8,1024]{1,0:T(8,128)S(1)}, f32[8,1024]{1,0:T(8,128)S(1)}, u32[]{:S(2)}, u32[]{:S(2)}) collective-permute-start(f32[8,1024]{1,0:T(8,128)S(1)} %bitcast.290), channel_id=1, source_target_pairs={{0,4},{4,8},{8,12},{12,16},{16,20},{20,24},{24,28},{1,5},{5,9},{9,... | collective-permute-start | bytes 98312 | tf_op jit(solution)/shard_map/ppermute | solution.py:30
  444.1 4.6 collective-permute-start.40
  445.4 4.7 collective-permute-start.39
  452.1 17.9 %copy-start.88 = (f32[10]{0:T(128)S(1)}, f32[10]{0:T(128)}, u32[]{:S(2)}) copy-start(f32[10]{0:T(128)} %copy-done.83) | copy-start | bytes 124
  478.8 10.8 %collective-permute-start.41 = (f32[10,1024]{1,0:T(8,128)S(1)}, f32[10,1024]{1,0:T(8,128)}, u32[]{:S(2)}, u32[]{:S(2)}) collective-permute-start(f32[10,1024]{1,0:T(8,128)S(1)} %bitcast.264), channel_id=1, source_target_pairs={{4,0},{8,4},{12,8},{16,12},{20,16},{24,20},{28,24},{5,1},{9,5},{13... | collective-permute-start | bytes 122888 | tf_op jit(solution)/shard_map/ppermute | solution.py:30
  (85 other events, 553.1 us)
